TPU v7x, 32 devices: a whole 2x2x4 slice. The times are simulated.
32 devices in a mesh: rep: 4 (over z), fsdp: 8 (over y, x, core).
Axes of the slice: x: 2, y: 2, z: 4, core: 2. Of those that a mesh axis runs over, the one named last changes fastest.
Arguments:
- tokens: bfloat16 [16384, 2048], P(('rep', 'fsdp')), may hold values from -6 to 6
- norm_gain: float32 [2048], replicated, may hold values from 0.5 to 1.5
- outer_params: float32 [2, 2048, 4096], P(None, 'fsdp'), may hold values from -6 to 6
- momentum: float32 [2, 2048, 4096], P(None, 'fsdp'), may hold values from -6 to 6
- deltas: bfloat16 [4, 2, 2048, 4096], P('rep', None, 'fsdp'), may hold values from -6 to 6
Outputs:
- new_params: float32 [2, 2048, 4096], P(None, 'fsdp')
- new_momentum: float32 [2, 2048, 4096], P(None, 'fsdp')
- hidden: bfloat16 [16384, 4096], P(('rep', 'fsdp'))
All inputs are finite; a program needn't handle non-finite values.
Results may differ from a plain program's by a relative error of at most 0.01.
Values may be sent and summed in bfloat16 or wider, within the bound.
A program may use at most 192 MiB of HBM per device.

v0:
```python
import functools
import math

import jax
import jax.numpy as jnp
from jax import lax
from jax.experimental import pallas as pl
from jax.experimental.pallas import tpu as pltpu
from jax.sharding import PartitionSpec as P

EPS = 1e-05
MU = 0.9
RATE = 0.7
CORES = 2
WIDTH = 256
SUM_LAG = 1
STEP_LAG = 2
SPLIT = 2


def advance(params, moment, summed, groups):
    outer_grad = summed * (1.0 / groups)
    moment_next = MU * moment + outer_grad
    params_next = params - RATE * (outer_grad + MU * moment_next)
    return (params_next, moment_next)


def kernel(
    groups, shards,
    tokens, gain, params, moment, deltas,
    p_out, m_out, hidden,
    full, own, peer_in, total, normed, h_slots,
    load_sem, token_sem, pm_sem, h_sem,
    part_recv, peer_recv, total_recv, ring_recv, pair_recv,
    part_send, total_send, ring_send, pair_send,
):
    chunks, pieces, low_height, width = own.shape
    split = pieces // 2
    height = low_height * split
    chips = shards // CORES
    half = chips // 2
    rows = normed.shape[0]
    rep = lax.axis_index("rep")
    mine = lax.axis_index("fsdp")
    core = mine % CORES
    chip = mine // CORES
    turn = half + chips - 1

    def flip(value):
        return value + (value // half) * (turn - 2 * value)

    place = flip(chip)

    def shard_at(position):
        return flip((position + chips) % chips) * CORES + core

    right, left = shard_at(place + 1), shard_at(place - 1)
    partner = chip * CORES + (1 - core)
    middle = groups // 2
    low = rep < middle
    inward = jnp.where(low, rep + 1, rep - 1)
    outward = jnp.where(low, rep - 1, rep + 1)
    at_end = (rep == 0) | (rep == groups - 1)
    at_middle = (rep == middle - 1) | (rep == middle)

    def columns(c):
        return pl.ds(pl.multiple_of(c * width, width), width)

    def block(c, which, owner):
        return full.at[c, which, pl.ds(pl.multiple_of(owner * height, height), height), :]

    def delta_load(c, q):
        at = pl.ds((q % split) * low_height, low_height)
        return pltpu.make_async_copy(deltas.at[0, q // split, at, columns(c)], own.at[c, q], load_sem.at[c])

    def state_loads(c):
        return (
            pltpu.make_async_copy(params.at[:, :, columns(c)], p_out.at[:, :, columns(c)], pm_sem.at[c % 2, 0]),
            pltpu.make_async_copy(moment.at[:, :, columns(c)], m_out.at[:, :, columns(c)], pm_sem.at[c % 2, 1]),
        )

    def part_copy(dst, c, q, recv):
        return pltpu.make_async_remote_copy(
            src_ref=own.at[c, q], dst_ref=dst.at[c, q], send_sem=part_send, recv_sem=recv.at[c, q],
            device_id={"rep": inward}, device_id_type=pl.DeviceIdType.MESH)

    def total_copy(c, q):
        return pltpu.make_async_remote_copy(
            src_ref=total.at[c, q], dst_ref=total.at[c, q], send_sem=total_send, recv_sem=total_recv.at[c, q],
            device_id={"rep": outward}, device_id_type=pl.DeviceIdType.MESH)

    def ring_copy(c, which, owner, hop, target):
        return pltpu.make_async_remote_copy(
            src_ref=block(c, which, owner), dst_ref=block(c, which, owner),
            send_sem=ring_send.at[which], recv_sem=ring_recv.at[c, which, hop - 1],
            device_id={"fsdp": target}, device_id_type=pl.DeviceIdType.MESH)

    def pair_copy(c, which, owner):
        return pltpu.make_async_remote_copy(
            src_ref=block(c, which, owner), dst_ref=block(c, which, owner),
            send_sem=pair_send, recv_sem=pair_recv.at[c],
            device_id={"fsdp": partner}, device_id_type=pl.DeviceIdType.MESH)

    @pl.loop(0, chunks)
    def _(c):
        for q in range(pieces):
            delta_load(c, q).start()

    token_copy = pltpu.make_async_copy(tokens, normed, token_sem)
    token_copy.start()
    for copy in state_loads(0):
        copy.start()

    barrier = pltpu.get_barrier_semaphore()
    for target in (partner, left, right):
        pl.semaphore_signal(barrier, inc=1, device_id={"fsdp": target}, device_id_type=pl.DeviceIdType.MESH)
    pl.semaphore_signal(barrier, inc=1, device_id={"rep": inward}, device_id_type=pl.DeviceIdType.MESH)

    @pl.when(jnp.logical_not(at_end))
    def _():
        pl.semaphore_signal(barrier, inc=1, device_id={"rep": outward}, device_id_type=pl.DeviceIdType.MESH)
        pl.semaphore_wait(barrier, 5)

    @pl.when(at_end)
    def _():
        pl.semaphore_wait(barrier, 4)

    @pl.loop(0, chunks)
    def _(c):
        pltpu.make_async_copy(own.at[c], own.at[c], load_sem.at[c]).wait()

        @pl.when(at_end & jnp.logical_not(at_middle))
        def _():
            for q in range(pieces):
                part_copy(total, c, q, part_recv).start()

        @pl.when(at_end & at_middle)
        def _():
            for q in range(pieces):
                part_copy(peer_in, c, q, peer_recv).start()

    token_copy.wait()
    piece = 64

    @pl.loop(0, rows // piece)
    def _(i):
        at = pl.ds(pl.multiple_of(i * piece, piece), piece)
        values = normed[at, :].astype(jnp.float32)
        scale = lax.rsqrt(jnp.mean(values * values, axis=-1, keepdims=True) + EPS)
        normed[at, :] = (values * scale * gain[...]).astype(jnp.bfloat16)

    factor = 1.0 / math.sqrt(normed.shape[1])
    last = chips - 1

    def live(c):
        return (c >= 0) & (c < chunks)

    @pl.loop(0, chunks + STEP_LAG + chips)
    def _(t):
        for hop in range(last, 0, -1):
            c = t - STEP_LAG - hop

            @pl.when(live(c))
            def _(c=c, hop=hop):
                for which, owner, target in ((0, shard_at(place - hop), right), (1, shard_at(place + hop), left)):
                    ring_copy(c, which, owner, hop, target).wait_recv()
                    if hop < last:
                        ring_copy(c, which, owner, hop + 1, target).start()
                    pair_copy(c, which, owner).start()

        u = t - STEP_LAG

        @pl.when(live(u))
        def _():
            @pl.when(u + 1 < chunks)
            def _():
                for copy in state_loads(u + 1):
                    copy.start()

            for copy in state_loads(u):
                copy.wait()
            for which, target in ((0, right), (1, left)):
                @pl.when(jnp.logical_not(at_middle))
                def _(which=which):
                    for q in range(which * split, (which + 1) * split):
                        total_copy(u, q).wait_recv()

                        @pl.when(jnp.logical_not(at_end))
                        def _(q=q):
                            total_copy(u, q).start()

                for q in range(which * split, (which + 1) * split):
                    rows_here = slice((q % split) * low_height, (q % split + 1) * low_height)
                    stepped, moved = advance(
                        p_out[which, rows_here, columns(u)], m_out[which, rows_here, columns(u)],
                        total[u, q].astype(jnp.float32), groups)
                    p_out[which, rows_here, columns(u)] = stepped
                    m_out[which, rows_here, columns(u)] = moved
                    start = mine * height + (q % split) * low_height
                    at = pl.ds(pl.multiple_of(start, low_height), low_height)
                    full[u, which, at, :] = stepped.astype(jnp.bfloat16)
                ring_copy(u, which, mine, 1, target).start()
                pair_copy(u, which, mine).start()

        s = t - SUM_LAG

        @pl.when(live(s) & at_middle)
        def _():
            for q in range(pieces):
                part_copy(peer_in, s, q, peer_recv).wait_recv()
                total[s, q] = (own[s, q].astype(jnp.float32) + peer_in[s, q].astype(jnp.float32)).astype(jnp.bfloat16)

                @pl.when(jnp.logical_not(at_end))
                def _(q=q):
                    total_copy(s, q).start()

        @pl.when((t < chunks) & jnp.logical_not(at_end))
        def _():
            for q in range(pieces):
                part_copy(total, t, q, part_recv).wait_recv()
                own[t, q] = (own[t, q].astype(jnp.float32) + total[t, q].astype(jnp.float32)).astype(jnp.bfloat16)

                @pl.when(at_middle)
                def _(q=q):
                    part_copy(peer_in, t, q, peer_recv).start()

                @pl.when(jnp.logical_not(at_middle))
                def _(q=q):
                    part_copy(total, t, q, part_recv).start()

        c = t - STEP_LAG - chips

        @pl.when(live(c))
        def _():
            arrived = full.at[c, :, 0:chips * height, :]
            pltpu.make_async_copy(arrived, arrived, pair_recv.at[c]).wait()
            slot = c % 2

            @pl.when(c >= 2)
            def _():
                pltpu.make_async_copy(h_slots.at[slot], hidden.at[:, columns(c)], h_sem.at[slot]).wait()

            tall = rows // 2

            @pl.loop(0, 2)
            def _(i):
                at = pl.ds(pl.multiple_of(i * tall, tall), tall)
                gate = jnp.dot(normed[at, :], full[c, 0], preferred_element_type=jnp.float32) * factor
                up = jnp.dot(normed[at, :], full[c, 1], preferred_element_type=jnp.float32) * factor
                h_slots[slot, at, :] = (gate / (1.0 + jnp.exp(-gate)) * up).astype(jnp.bfloat16)

            pltpu.make_async_copy(h_slots.at[slot], hidden.at[:, columns(c)], h_sem.at[slot]).start()

    for slot in range(2):
        pltpu.make_async_copy(h_slots.at[slot], hidden.at[:, columns(0)], h_sem.at[slot]).wait()
    pltpu.make_async_copy(own, own, part_send).wait()

    @pl.when(jnp.logical_not(at_end))
    def _():
        pltpu.make_async_copy(total, total, total_send).wait()

    for which in range(2):
        sent = full.at[:, which, 0:last * height, :]
        pltpu.make_async_copy(sent, sent, ring_send.at[which]).wait()
    sent = full.at[:, :, 0:chips * height, :]
    pltpu.make_async_copy(sent, sent, pair_send).wait()


def solution(mesh):
    groups, shards = mesh.shape["rep"], mesh.shape["fsdp"]
    chips = shards // CORES

    def body(tokens, norm_gain, outer_params, momentum, deltas):
        rows, model = tokens.shape
        _, height, hid = outer_params.shape
        width = WIDTH
        chunks = hid // width
        bf16, f32 = jnp.bfloat16, jnp.float32
        dma = pltpu.SemaphoreType.DMA
        strip = pltpu.VMEM((chunks, 2 * SPLIT, height // SPLIT, width), bf16)
        each = dma((chunks, 2 * SPLIT))
        anywhere = pl.BlockSpec(memory_space=pl.ANY)
        new_params, new_momentum, hidden = pl.pallas_call(
            functools.partial(kernel, groups, shards),
            out_shape=(
                pltpu.VMEM(outer_params.shape, f32),
                pltpu.VMEM(outer_params.shape, f32),
                jax.ShapeDtypeStruct((rows, hid), bf16),
            ),
            in_specs=[anywhere, pl.BlockSpec(memory_space=pltpu.VMEM), anywhere, anywhere, anywhere],
            out_specs=(pl.BlockSpec(memory_space=pltpu.VMEM), pl.BlockSpec(memory_space=pltpu.VMEM), anywhere),
            scratch_shapes=[
                pltpu.VMEM((chunks, 2, model, width), bf16),
                strip, strip, strip,
                pltpu.VMEM((rows, model), bf16),
                pltpu.VMEM((2, rows, width), bf16),
                dma((chunks,)), dma, dma((2, 2)), dma((2,)),
                each, each, each, dma((chunks, 2, chips - 1)), dma((chunks,)),
                dma, dma, dma((2,)), dma,
            ],
            compiler_params=pltpu.CompilerParams(
                collective_id=0, has_side_effects=True, vmem_limit_bytes=191 * 256 * 1024),
            name="round",
        )(tokens, norm_gain.reshape(1, model), outer_params, momentum, deltas)
        return (new_params, new_momentum, hidden)

    in_specs = (
        P(("rep", "fsdp"), None),
        P(),
        P(None, "fsdp", None),
        P(None, "fsdp", None),
        P("rep", None, "fsdp", None),
    )
    out_specs = (P(None, "fsdp", None), P(None, "fsdp", None), P(("rep", "fsdp"), None))
    return jax.shard_map(body, mesh=mesh, in_specs=in_specs, out_specs=out_specs, check_vma=False)
```

profile of v0, /device:TPU:0, one launch (start us, length us, event | category | flops | bytes accessed | tf_op | source)
XLA Modules:
  0.0 178.4 jit_solution(2165185484887914633)
XLA Ops:
  0.6 167.1 %round.1 = (f32[2,256,4096]{2,1,0:T(8,128)S(1)}, f32[2,256,4096]{2,1,0:T(8,128)S(1)}, bf16[512,4096]{1,0:T(8,128)(2,1)}) custom-call(bf16[512,2048]{1,0:T(8,128)(2,1)} %tokens.1, f32[1,2048]{1,0:T(1,128)} %bitcast.1, f32[2,256,4096]{2,1,0:T(8,128)} %params.1, f32[2,256,4096]{2,1,0:T(8,128)} %moment.1, bf16[1,2,256,4096]{3,2,1,0:T(8,128)(2,1)} %deltas.1), custom_call_target="tpu_custom_call" | custom-call | tf_op jit(solution)/shard_map/round/pallas_call | solution.py:283
  167.8 3.4 %copy.11 = f32[2,256,4096]{2,1,0:T(8,128)} copy(f32[2,256,4096]{2,1,0:T(8,128)S(1)} %get-tuple-element.3) | data formatting | bytes 16777216
  171.2 0.0 copy-start
  171.2 4.3 %copy.12 = f32[2,256,4096]{2,1,0:T(8,128)} copy(f32[2,256,4096]{2,1,0:T(8,128)S(1)} %get-tuple-element.4) | data formatting | bytes 16777216
  175.4 1.0 copy-done
  176.4 2.0 %copy.13 = bf16[512,4096]{1,0:T(8,128)(2,1)} copy(bf16[512,4096]{1,0:T(8,128)(2,1)S(1)} %copy-done) | data formatting | bytes 8388608
Async XLA Ops:
  171.2 5.2 %copy-start = (bf16[512,4096]{1,0:T(8,128)(2,1)S(1)}, bf16[512,4096]{1,0:T(8,128)(2,1)}, u32[]{:S(2)}) copy-start(bf16[512,4096]{1,0:T(8,128)(2,1)} %get-tuple-element.11) | copy-start | bytes 12582916
where the time goes:
time: 179 us; the launch traced here: 178 us
  Pallas kernels  167 us (93%)
  local copies, waits for them, and re-layouts  10.6 us (6%)
    pallas_call x1, Pallas kernels, body(): pl.pallas_call(functools.partial(kernel, groups, shards), out_shape=(pltp...  167 us
    unnamed x5, local copies, waits for them, and re-layouts  10.6 us

commit v1 on v0

v1 whole, which is shorter than its diff:
```python
import functools
import math

import jax
import jax.numpy as jnp
from jax import lax
from jax.experimental import pallas as pl
from jax.experimental.pallas import tpu as pltpu
from jax.sharding import PartitionSpec as P

EPS = 1e-05
MU = 0.9
RATE = 0.7
CORES = 2
LANES = 4
WIDTH = 128
PARTS = 4
EARLY = 3
LATE_AT = 4
PASS_AT = (4, 7, 10, 14)
SUM_LAG = 1
STEP_LAG = 2
PASS_LAG = 5
DOT_LAG = 4


def advance(params, moment, summed, groups):
    outer_grad = summed * (1.0 / groups)
    moment_next = MU * moment + outer_grad
    params_next = params - RATE * (outer_grad + MU * moment_next)
    return (params_next, moment_next)


def other(bit, turned):
    return 1 - bit if turned else bit


def kernel(
    groups, shards, z_rows,
    tokens, gain, params, moment, deltas,
    p_out, m_out, hid_out,
    toks, weights, stage, own, peer_in, total, h_x, h_z,
    load_sem, token_sem, p_sem, m_sem,
    part_recv, peer_recv, total_recv, part_send, total_send,
    tx_recv, tx_send, tz_recv, tz_send, pair_recv, diag_recv, pair_send,
    lane_recv, lane_send, far_recv, far_send, h_recv, h_send,
):
    pieces, _, height, width = own.shape
    chunks = pieces // LANES
    rows, model = tokens.shape
    x_rows = rows - z_rows
    z_base = LANES * x_rows
    quarter = chunks * width
    quads = shards // LANES
    bf16, f32 = jnp.bfloat16, jnp.float32
    rep = lax.axis_index("rep")
    mine = lax.axis_index("fsdp")
    core = mine % CORES
    chip = mine // CORES
    x_bit = chip % 2
    quad = chip // 2
    turn = ((rep + 1) // 2) % 2
    lane = ((x_bit + turn) % 2) * 2 + core
    middle = groups // 2
    low = rep < middle
    inward = jnp.where(low, rep + 1, rep - 1)
    outward = jnp.where(low, rep - 1, rep + 1)
    at_end = (rep == 0) | (rep == groups - 1)
    at_middle = (rep == middle - 1) | (rep == middle)
    z_pair = rep + 1 - 2 * (rep % 2)

    def shard(bit, which_core, where=quad):
        return (where * 2 + bit) * CORES + which_core

    def at_x(k):
        return shard(other(x_bit, k // 2), other(core, k % 2))

    def remote(src, dst, send, recv, **device):
        return pltpu.make_async_remote_copy(
            src_ref=src, dst_ref=dst, send_sem=send, recv_sem=recv,
            device_id=device, device_id_type=pl.DeviceIdType.MESH)

    def z_device(k):
        near = {"fsdp": chip * CORES + other(core, k % 2)}
        return {"rep": z_pair, **near} if k // 2 else near

    def high(i):
        return (LANES - 1 - i) // 2

    def odd(i):
        return (LANES - 1 - i) % 2

    def columns(c, i):
        h = other(x_bit, high(i)) * 2 + other(core, odd(i))
        return pl.ds(pl.multiple_of(h * quarter + c * width, width), width)

    def away(i):
        return (high(i) + turn) % 2

    def lane_shard(i, where=quad):
        return shard((x_bit + high(i) + turn) % 2, other(core, odd(i)), where)

    def block(c, owner):
        return weights.at[c, pl.ds(pl.multiple_of(owner * height, height), height), :]

    def delta_load(c, i):
        n = c * LANES + i
        return pltpu.make_async_copy(deltas.at[0, :, :, columns(c, i)], own.at[n], load_sem.at[n])

    def part_copy(dst, n, recv):
        return remote(own.at[n], dst.at[n], part_send, recv.at[n], rep=inward)

    def total_copy(n):
        return remote(total.at[n], total.at[n], total_send, total_recv.at[n], rep=outward)

    def lane_copy(c, i):
        return remote(stage.at[c * LANES + i], block(c, mine), lane_send, lane_recv.at[c, i], fsdp=lane_shard(i))

    def far_copy(c, i, r):
        at = block(c, lane_shard(i))
        return remote(at, at, far_send, far_recv.at[c], fsdp=shard(x_bit, core, (quad + r) % quads))

    part_rows = x_rows // PARTS

    def x_part(k, j):
        return toks.at[pl.ds(k * x_rows + j * part_rows, part_rows), :]

    def z_part(k):
        return toks.at[pl.ds(z_base + k * z_rows, z_rows), :]

    def token_x(j):
        return remote(x_part(0, j), x_part(2, j), tx_send, tx_recv.at[j], fsdp=at_x(2))

    def token_pass(j):
        return remote(x_part(2, j), x_part(3, j), pair_send, diag_recv.at[0], fsdp=at_x(1))

    def token_z():
        return remote(z_part(0), z_part(2), tz_send, tz_recv, rep=z_pair)

    def token_z_pass():
        return remote(z_part(2), z_part(3), pair_send, diag_recv.at[1], fsdp=at_x(1))

    token_copies = (
        pltpu.make_async_copy(tokens.at[pl.ds(0, x_rows), :], toks.at[pl.ds(0, x_rows), :], token_sem.at[0]),
        pltpu.make_async_copy(tokens.at[pl.ds(x_rows, z_rows), :], z_part(0), token_sem.at[1]),
    )
    for copy in token_copies:
        copy.start()

    @pl.loop(0, chunks)
    def _(c):
        for i in range(LANES):
            delta_load(c, i).start()

    p_load = pltpu.make_async_copy(params, p_out, p_sem)
    m_load = pltpu.make_async_copy(moment, m_out, m_sem)
    p_load.start()
    m_load.start()

    barrier = pltpu.get_barrier_semaphore()
    greeted = 0
    for k in (1, 2, 3):
        pl.semaphore_signal(barrier, inc=1, device_id={"fsdp": at_x(k)}, device_id_type=pl.DeviceIdType.MESH)
    for r in range(1, quads):
        pl.semaphore_signal(
            barrier, inc=1, device_id={"fsdp": shard(x_bit, core, (quad + r) % quads)}, device_id_type=pl.DeviceIdType.MESH)
    pl.semaphore_signal(barrier, inc=1, device_id=z_device(3), device_id_type=pl.DeviceIdType.MESH)
    pl.semaphore_signal(barrier, inc=1, device_id={"rep": inward}, device_id_type=pl.DeviceIdType.MESH)
    greeted = LANES - 1 + quads - 1 + 2

    @pl.when(jnp.logical_not(at_end))
    def _():
        pl.semaphore_signal(barrier, inc=1, device_id={"rep": outward}, device_id_type=pl.DeviceIdType.MESH)

    for copy in token_copies:
        copy.wait()
    piece = 32

    def normalize(first, count):
        @pl.loop(0, count // piece)
        def _(i):
            at = pl.ds(pl.multiple_of(first + i * piece, piece), piece)
            values = toks[at, :].astype(f32)
            scale = lax.rsqrt(jnp.mean(values * values, axis=-1, keepdims=True) + EPS)
            toks[at, :] = (values * scale * gain[...]).astype(bf16)

    normalize(0, x_rows)
    normalize(z_base, z_rows)

    @pl.when(jnp.logical_not(at_end))
    def _():
        pl.semaphore_wait(barrier, greeted + 1)

    @pl.when(at_end)
    def _():
        pl.semaphore_wait(barrier, greeted)

    for j in range(EARLY):
        token_x(j).start()

    @pl.when(jnp.logical_not(at_end))
    def _():
        token_z().start()

    @pl.loop(0, chunks)
    def _(c):
        for i in range(LANES):
            n = c * LANES + i
            pltpu.make_async_copy(own.at[n], own.at[n], load_sem.at[n]).wait()

            @pl.when(at_end & jnp.logical_not(at_middle))
            def _(n=n):
                part_copy(total, n, part_recv).start()

            @pl.when(at_end & at_middle)
            def _(n=n):
                part_copy(peer_in, n, peer_recv).start()

    @pl.when(at_end)
    def _():
        token_z().start()

    remote(toks.at[pl.ds(0, x_rows), :], toks.at[pl.ds(x_rows, x_rows), :], pair_send, pair_recv.at[0], fsdp=at_x(1)).start()
    remote(z_part(0), z_part(1), pair_send, pair_recv.at[1], fsdp=at_x(1)).start()

    factor = 1.0 / math.sqrt(model)

    def gated(at, c):
        both = jnp.dot(toks[at, :], weights[c], preferred_element_type=f32) * factor
        gate, up = both[:, :width], both[:, width:]
        return (gate / (1.0 + jnp.exp(-gate)) * up).astype(bf16)

    def live(c):
        return (c >= 0) & (c < chunks)

    def shifted(t, i, lag):
        return t + (i - lag) // LANES, (i - lag) % LANES

    def gather_in(c, i):
        n = c * LANES + i
        part_copy(total, n, part_recv).wait_recv()
        own[n] = (own[n].astype(f32) + total[n].astype(f32)).astype(bf16)

        @pl.when(at_middle)
        def _():
            part_copy(peer_in, n, peer_recv).start()

        @pl.when(jnp.logical_not(at_middle))
        def _():
            part_copy(total, n, part_recv).start()

    def join(c, i):
        n = c * LANES + i
        part_copy(peer_in, n, peer_recv).wait_recv()
        total[n] = (own[n].astype(f32) + peer_in[n].astype(f32)).astype(bf16)

        @pl.when(jnp.logical_not(at_end))
        def _():
            total_copy(n).start()

    def update(c, i):
        n = c * LANES + i

        @pl.when(jnp.logical_not(at_middle))
        def _():
            total_copy(n).wait_recv()

            @pl.when(jnp.logical_not(at_end))
            def _():
                total_copy(n).start()

        if i == 0:
            @pl.when(c == 0)
            def _():
                p_load.wait()
                m_load.wait()

        at = columns(c, i)
        for which in range(2):
            stepped, moved = advance(p_out[which, :, at], m_out[which, :, at], total[n, which].astype(f32), groups)
            p_out[which, :, at] = stepped
            m_out[which, :, at] = moved
            stage[n, :, which * width:(which + 1) * width] = stepped.astype(bf16)
        if odd(i):
            lane_copy(c, i).start()
        else:
            @pl.when(away(i) == 1)
            def _():
                lane_copy(c, i).start()

            @pl.when(away(i) == 0)
            def _():
                start = pl.multiple_of(mine * height, height)
                weights[c, pl.ds(start, height), :] = stage[n]

    def pass_on(c, i):
        if odd(i):
            lane_copy(c, i).wait_recv()
        else:
            @pl.when(away(i) == 1)
            def _():
                lane_copy(c, i).wait_recv()
        for r in range(1, quads):
            far_copy(c, i, r).start()

    def project(c, k):
        hidden = gated(slice(k * x_rows, (k + 1) * x_rows), c)
        slot = lane * chunks + c
        if k == 0:
            hid_out[slot, 0:x_rows, :] = hidden
        else:
            h_x[c, k - 1] = hidden
            remote(h_x.at[c, k - 1], hid_out.at[slot, pl.ds(0, x_rows), :], h_send.at[0], h_recv.at[0], fsdp=at_x(k)).start()

    def project_z(c):
        hidden = gated(slice(z_base, z_base + LANES * z_rows), c)
        slot = lane * chunks + c
        hid_out[slot, x_rows:rows, :] = hidden[0:z_rows]
        h_z[c] = hidden[z_rows:]
        for k in (3, 2, 1):
            remote(h_z.at[c, pl.ds((k - 1) * z_rows, z_rows), :], hid_out.at[slot, pl.ds(x_rows, z_rows), :],
                   h_send.at[1], h_recv.at[1], **z_device(k)).start()

    tail_z = -(-chunks // DOT_LAG)

    @pl.loop(0, chunks + DOT_LAG)
    def _(t):
        for i in range(LANES):
            @pl.when((t < chunks) & jnp.logical_not(at_end))
            def _(i=i):
                gather_in(t, i)

            for stepper, lag, when in ((join, SUM_LAG, at_middle), (update, STEP_LAG, None), (pass_on, PASS_LAG, None)):
                c, at = shifted(t, i, lag)

                @pl.when(live(c) if when is None else live(c) & when)
                def _(stepper=stepper, c=c, at=at):
                    stepper(c, at)

            if LATE_AT % LANES == i:
                @pl.when(t == LATE_AT // LANES)
                def _():
                    for j in range(EARLY, PARTS):
                        token_x(j).start()

            for j in range(PARTS):
                if PASS_AT[j] % LANES == i:
                    @pl.when(t == PASS_AT[j] // LANES)
                    def _(j=j):
                        token_x(j).wait_recv()
                        token_pass(j).start()

            @pl.when(live(t - DOT_LAG))
            def _(i=i):
                c = t - DOT_LAG
                if i == 0:
                    @pl.when(c == 0)
                    def _():
                        there = toks.at[pl.ds(x_rows, x_rows), :]
                        pltpu.make_async_copy(there, there, pair_recv.at[0]).wait()
                        pltpu.make_async_copy(there, there, diag_recv.at[0]).wait()

                    for _ in range(1, quads):
                        arrived = weights.at[c, pl.ds(0, LANES * height), :]
                        pltpu.make_async_copy(arrived, arrived, far_recv.at[c]).wait()
                project(c, LANES - 1 - i)

        @pl.when(t == chunks)
        def _():
            token_z().wait_recv()
            token_z_pass().start()
            pltpu.make_async_copy(z_part(1), z_part(1), pair_recv.at[1]).wait()
            pltpu.make_async_copy(z_part(3), z_part(3), diag_recv.at[1]).wait()

        @pl.when(t >= chunks)
        def _():
            first = (t - chunks) * tail_z

            @pl.loop(first, jnp.minimum(first + tail_z, chunks))
            def _(c):
                project_z(c)

    got = hid_out.at[pl.ds(0, (LANES - 1) * chunks), pl.ds(0, x_rows), :]
    pltpu.make_async_copy(got, got, h_recv.at[0]).wait()
    got = hid_out.at[pl.ds(0, (LANES - 1) * chunks), pl.ds(x_rows, z_rows), :]
    pltpu.make_async_copy(got, got, h_recv.at[1]).wait()
    pltpu.make_async_copy(h_x, h_x, h_send.at[0]).wait()
    pltpu.make_async_copy(h_z, h_z, h_send.at[1]).wait()
    pltpu.make_async_copy(own, own, part_send).wait()

    @pl.when(jnp.logical_not(at_end))
    def _():
        pltpu.make_async_copy(total, total, total_send).wait()

    sent = stage.at[pl.ds(0, (LANES - 1) * chunks)]
    pltpu.make_async_copy(sent, sent, lane_send).wait()
    for _ in range(1, quads):
        pltpu.make_async_copy(stage, stage, far_send).wait()
    sent = toks.at[pl.ds(0, x_rows), :]
    pltpu.make_async_copy(sent, sent, tx_send).wait()
    pltpu.make_async_copy(z_part(0), z_part(0), tz_send).wait()
    sent = toks.at[pl.ds(0, 2 * rows), :]
    pltpu.make_async_copy(sent, sent, pair_send).wait()


def store(p_in, m_in, h_in, p_out, m_out, hidden, p_sem, m_sem, h_sem):
    blocks, _, width = h_in.shape
    p_copy = pltpu.make_async_copy(p_in, p_out, p_sem)
    m_copy = pltpu.make_async_copy(m_in, m_out, m_sem)
    for j in range(blocks):
        pltpu.make_async_copy(h_in.at[j], hidden.at[:, pl.ds(j * width, width)], h_sem).start()
    p_copy.start()
    m_copy.start()
    pltpu.make_async_copy(h_in, h_in, h_sem).wait()
    p_copy.wait()
    m_copy.wait()


def solution(mesh):
    groups, shards = mesh.shape["rep"], mesh.shape["fsdp"]

    def body(tokens, norm_gain, outer_params, momentum, deltas):
        rows, model = tokens.shape
        _, height, hid = outer_params.shape
        width = WIDTH
        chunks = hid // (LANES * width)
        pieces = chunks * LANES
        z_rows = rows // 4
        x_rows = rows - z_rows
        bf16, f32 = jnp.bfloat16, jnp.float32
        dma = pltpu.SemaphoreType.DMA
        strip = pltpu.VMEM((pieces, 2, height, width), bf16)
        anywhere = pl.BlockSpec(memory_space=pl.ANY)
        inside = pl.BlockSpec(memory_space=pltpu.VMEM)
        new_params, new_momentum, blocks = pl.pallas_call(
            functools.partial(kernel, groups, shards, z_rows),
            out_shape=(
                pltpu.VMEM(outer_params.shape, f32),
                pltpu.VMEM(outer_params.shape, f32),
                pltpu.VMEM((pieces, rows, width), bf16),
            ),
            in_specs=[anywhere, inside, anywhere, anywhere, anywhere],
            out_specs=(inside, inside, inside),
            scratch_shapes=[
                pltpu.VMEM((LANES * rows, model), bf16),
                pltpu.VMEM((chunks, model, 2 * width), bf16),
                pltpu.VMEM((pieces, height, 2 * width), bf16),
                strip, strip, strip,
                pltpu.VMEM((chunks, LANES - 1, x_rows, width), bf16),
                pltpu.VMEM((chunks, (LANES - 1) * z_rows, width), bf16),
                dma((pieces,)), dma((2,)), dma, dma,
                dma((pieces,)), dma((pieces,)), dma((pieces,)), dma, dma,
                dma((PARTS,)), dma, dma, dma, dma((2,)), dma((2,)), dma,
                dma((chunks, LANES)), dma, dma((chunks,)), dma, dma((2,)), dma((2,)),
            ],
            compiler_params=pltpu.CompilerParams(
                collective_id=0, has_side_effects=True, vmem_limit_bytes=175 * 256 * 1024),
            name="round",
        )(tokens, norm_gain.reshape(1, model), outer_params, momentum, deltas)
        return pl.pallas_call(
            store,
            out_shape=(
                jax.ShapeDtypeStruct(outer_params.shape, f32),
                jax.ShapeDtypeStruct(outer_params.shape, f32),
                jax.ShapeDtypeStruct((rows, hid), bf16),
            ),
            in_specs=[inside, inside, inside],
            out_specs=(anywhere, anywhere, anywhere),
            scratch_shapes=[dma, dma, dma],
            compiler_params=pltpu.CompilerParams(vmem_limit_bytes=22 * 1024 * 1024),
            name="store",
        )(new_params, new_momentum, blocks)

    in_specs = (
        P(("rep", "fsdp"), None),
        P(),
        P(None, "fsdp", None),
        P(None, "fsdp", None),
        P("rep", None, "fsdp", None),
    )
    out_specs = (P(None, "fsdp", None), P(None, "fsdp", None), P(("rep", "fsdp"), None))
    return jax.shard_map(body, mesh=mesh, in_specs=in_specs, out_specs=out_specs, check_vma=False)
```

time: 179 us -> 151 us (0.84)
  Pallas kernels: 167 us -> 150 us
  local copies, waits for them, and re-layouts: 10.6 us -> 0 us
    pallas_call x1 -> x2, Pallas kernels: 167 us -> 150 us  [the longest x1 143 us: body(): pl.pallas_call(functools.partial(kernel, groups, shards, z_rows), out_sha...]
    unnamed x5 -> x0, local copies, waits for them, and re-layouts: 10.6 us -> none
where the time goes in v1:
time: 151 us
  Pallas kernels  150 us (99%)
    pallas_call x1, Pallas kernels, body(): pl.pallas_call(functools.partial(kernel, groups, shards, z_rows), out_sha...  143 us
    pallas_call x1, Pallas kernels, body(): pl.pallas_call(store, out_shape=(jax.ShapeDtypeStruct(outer_params.shape,...  7.31 us

profile of v1, /device:TPU:0, one launch (start us, length us, event | category | flops | bytes accessed | tf_op | source)
XLA Modules:
  0.0 150.8 jit_solution(1283054454196596127)
XLA Ops:
  0.6 142.8 %round.1 = (f32[2,256,4096]{2,1,0:T(8,128)S(1)}, f32[2,256,4096]{2,1,0:T(8,128)S(1)}, bf16[32,512,128]{2,1,0:T(8,128)(2,1)S(1)}) custom-call(bf16[512,2048]{1,0:T(8,128)(2,1)} %tokens.1, f32[1,2048]{1,0:T(1,128)} %bitcast.1, f32[2,256,4096]{2,1,0:T(8,128)} %params.1, f32[2,256,4096]{2,1,0:T(8,128)} %moment.1, bf16[1,2,256,4096]{3,2,1,0:T(8,128)(2,1)} %deltas.1), custom_call_target="tpu_custom_call" | custom-call | tf_op jit(solution)/shard_map/round/pallas_call | solution.py:435
  143.4 7.3 %store.1 = (f32[2,256,4096]{2,1,0:T(8,128)}, f32[2,256,4096]{2,1,0:T(8,128)}, bf16[512,4096]{1,0:T(8,128)(2,1)}) custom-call(f32[2,256,4096]{2,1,0:T(8,128)S(1)} %get-tuple-element.6.p_in, f32[2,256,4096]{2,1,0:T(8,128)S(1)} %get-tuple-element.7.m_in, bf16[32,512,128]{2,1,0:T(8,128)(2,1)S(1)} %get-tuple-element.8.h_in), custom_call_target="tpu_custom_call" | custom-call | tf_op jit(solution)/shard_map/store/pallas_call | solution.py:460

commit v2 on v1

--- a/solution.py
+++ b/solution.py
@@ -14,14 +14,15 @@
 CORES = 2
 LANES = 4
 WIDTH = 128
-PARTS = 4
-EARLY = 3
-LATE_AT = 4
-PASS_AT = (4, 7, 10, 14)
+PARTS = 6
+SEND_AT = ((None, None, None, None, 5, 9), (None, None, 3, 7, 11, 15))
+PASS_AT = ((2, 4, 6, 8, 10, 13), (2, 4, 8, 12, 15, 19))
+DOT_AT = (14, 20)
 SUM_LAG = 1
 STEP_LAG = 2
-PASS_LAG = 5
-DOT_LAG = 4
+NEAR_LAG = 4
+FAR_LAG = 5
+DOT_LAG = 12
 
 
 def advance(params, moment, summed, groups):
@@ -84,21 +85,21 @@
         near = {"fsdp": chip * CORES + other(core, k % 2)}
         return {"rep": z_pair, **near} if k // 2 else near
 
-    def high(i):
-        return (LANES - 1 - i) // 2
-
-    def odd(i):
-        return (LANES - 1 - i) % 2
+    def order(c, i):
+        return jnp.where(c < chunks // 2, i, LANES - 1 - i)
 
     def columns(c, i):
-        h = other(x_bit, high(i)) * 2 + other(core, odd(i))
+        at = order(c, i)
+        h = (x_bit + at // 2) % 2 * 2 + (core + at % 2) % 2
         return pl.ds(pl.multiple_of(h * quarter + c * width, width), width)
 
-    def away(i):
-        return (high(i) + turn) % 2
-
-    def lane_shard(i, where=quad):
-        return shard((x_bit + high(i) + turn) % 2, other(core, odd(i)), where)
+    def relative(c, i):
+        at = order(c, i)
+        return (at // 2 + turn) % 2, at % 2
+
+    def lane_shard(c, i):
+        far, near = relative(c, i)
+        return shard((x_bit + far) % 2, (core + near) % 2)
 
     def block(c, owner):
         return weights.at[c, pl.ds(pl.multiple_of(owner * height, height), height), :]
@@ -114,10 +115,10 @@
         return remote(total.at[n], total.at[n], total_send, total_recv.at[n], rep=outward)
 
     def lane_copy(c, i):
-        return remote(stage.at[c * LANES + i], block(c, mine), lane_send, lane_recv.at[c, i], fsdp=lane_shard(i))
+        return remote(stage.at[c * LANES + i], block(c, mine), lane_send, lane_recv.at[c, i], fsdp=lane_shard(c, i))
 
     def far_copy(c, i, r):
-        at = block(c, lane_shard(i))
+        at = block(c, lane_shard(c, i))
         return remote(at, at, far_send, far_recv.at[c], fsdp=shard(x_bit, core, (quad + r) % quads))
 
     part_rows = x_rows // PARTS
@@ -125,8 +126,10 @@
     def x_part(k, j):
         return toks.at[pl.ds(k * x_rows + j * part_rows, part_rows), :]
 
-    def z_part(k):
-        return toks.at[pl.ds(z_base + k * z_rows, z_rows), :]
+    def z_part(k, half=None):
+        if half is None:
+            return toks.at[pl.ds(z_base + k * z_rows, z_rows), :]
+        return toks.at[pl.ds(z_base + k * z_rows + half * (z_rows // 2), z_rows // 2), :]
 
     def token_x(j):
         return remote(x_part(0, j), x_part(2, j), tx_send, tx_recv.at[j], fsdp=at_x(2))
@@ -134,24 +137,25 @@
     def token_pass(j):
         return remote(x_part(2, j), x_part(3, j), pair_send, diag_recv.at[0], fsdp=at_x(1))
 
-    def token_z():
-        return remote(z_part(0), z_part(2), tz_send, tz_recv, rep=z_pair)
+    def token_z(half):
+        return remote(z_part(0, half), z_part(2, half), tz_send, tz_recv, rep=z_pair)
 
     def token_z_pass():
         return remote(z_part(2), z_part(3), pair_send, diag_recv.at[1], fsdp=at_x(1))
-
-    token_copies = (
-        pltpu.make_async_copy(tokens.at[pl.ds(0, x_rows), :], toks.at[pl.ds(0, x_rows), :], token_sem.at[0]),
-        pltpu.make_async_copy(tokens.at[pl.ds(x_rows, z_rows), :], z_part(0), token_sem.at[1]),
-    )
-    for copy in token_copies:
-        copy.start()
 
     @pl.loop(0, chunks)
     def _(c):
         for i in range(LANES):
             delta_load(c, i).start()
 
+    token_copies = [
+        pltpu.make_async_copy(
+            tokens.at[pl.ds(j * part_rows, part_rows), :], x_part(0, j), token_sem.at[j])
+        for j in range(PARTS)
+    ]
+    token_copies.append(pltpu.make_async_copy(tokens.at[pl.ds(x_rows, z_rows), :], z_part(0), token_sem.at[PARTS]))
+    for copy in token_copies:
+        copy.start()
     p_load = pltpu.make_async_copy(params, p_out, p_sem)
     m_load = pltpu.make_async_copy(moment, m_out, m_sem)
     p_load.start()
@@ -172,8 +176,26 @@
     def _():
         pl.semaphore_signal(barrier, inc=1, device_id={"rep": outward}, device_id_type=pl.DeviceIdType.MESH)
 
-    for copy in token_copies:
-        copy.wait()
+    @pl.when(jnp.logical_not(at_end))
+    def _():
+        pl.semaphore_wait(barrier, greeted + 1)
+
+    @pl.when(at_end)
+    def _():
+        pl.semaphore_wait(barrier, greeted)
+
+    @pl.loop(0, pieces)
+    def _(n):
+        pltpu.make_async_copy(own.at[n], own.at[n], load_sem.at[n]).wait()
+
+        @pl.when(at_end & jnp.logical_not(at_middle))
+        def _():
+            part_copy(total, n, part_recv).start()
+
+        @pl.when(at_end & at_middle)
+        def _():
+            part_copy(peer_in, n, peer_recv).start()
+
     piece = 32
 
     def normalize(first, count):
@@ -184,41 +206,24 @@
             scale = lax.rsqrt(jnp.mean(values * values, axis=-1, keepdims=True) + EPS)
             toks[at, :] = (values * scale * gain[...]).astype(bf16)
 
-    normalize(0, x_rows)
+    for j in range(PARTS):
+        token_copies[j].wait()
+        normalize(j * part_rows, part_rows)
+        early = [role[j] is None for role in SEND_AT]
+        if all(early):
+            token_x(j).start()
+        elif any(early):
+            @pl.when(at_end if early[0] else jnp.logical_not(at_end))
+            def _(j=j):
+                token_x(j).start()
+
+    token_copies[PARTS].wait()
     normalize(z_base, z_rows)
-
-    @pl.when(jnp.logical_not(at_end))
-    def _():
-        pl.semaphore_wait(barrier, greeted + 1)
+    token_z(0).start()
 
     @pl.when(at_end)
     def _():
-        pl.semaphore_wait(barrier, greeted)
-
-    for j in range(EARLY):
-        token_x(j).start()
-
-    @pl.when(jnp.logical_not(at_end))
-    def _():
-        token_z().start()
-
-    @pl.loop(0, chunks)
-    def _(c):
-        for i in range(LANES):
-            n = c * LANES + i
-            pltpu.make_async_copy(own.at[n], own.at[n], load_sem.at[n]).wait()
-
-            @pl.when(at_end & jnp.logical_not(at_middle))
-            def _(n=n):
-                part_copy(total, n, part_recv).start()
-
-            @pl.when(at_end & at_middle)
-            def _(n=n):
-                part_copy(peer_in, n, peer_recv).start()
-
-    @pl.when(at_end)
-    def _():
-        token_z().start()
+        token_z(1).start()
 
     remote(toks.at[pl.ds(0, x_rows), :], toks.at[pl.ds(x_rows, x_rows), :], pair_send, pair_recv.at[0], fsdp=at_x(1)).start()
     remote(z_part(0), z_part(1), pair_send, pair_recv.at[1], fsdp=at_x(1)).start()
@@ -276,41 +281,66 @@
                 m_load.wait()
 
         at = columns(c, i)
+        far, near = relative(c, i)
+        kept = (far == 0) & (near == 0)
         for which in range(2):
             stepped, moved = advance(p_out[which, :, at], m_out[which, :, at], total[n, which].astype(f32), groups)
             p_out[which, :, at] = stepped
             m_out[which, :, at] = moved
             stage[n, :, which * width:(which + 1) * width] = stepped.astype(bf16)
-        if odd(i):
+
+        @pl.when(jnp.logical_not(kept))
+        def _():
             lane_copy(c, i).start()
-        else:
-            @pl.when(away(i) == 1)
-            def _():
-                lane_copy(c, i).start()
-
-            @pl.when(away(i) == 0)
-            def _():
-                start = pl.multiple_of(mine * height, height)
-                weights[c, pl.ds(start, height), :] = stage[n]
-
-    def pass_on(c, i):
-        if odd(i):
+
+        @pl.when(kept)
+        def _():
+            start = pl.multiple_of(mine * height, height)
+            weights[c, pl.ds(start, height), :] = stage[n]
+            for r in range(1, quads):
+                far_copy(c, i, r).start()
+
+    def pass_on(c, i, from_far):
+        far, near = relative(c, i)
+
+        @pl.when((far == 1) if from_far else (far == 0) & (near == 1))
+        def _():
             lane_copy(c, i).wait_recv()
-        else:
-            @pl.when(away(i) == 1)
-            def _():
-                lane_copy(c, i).wait_recv()
-        for r in range(1, quads):
-            far_copy(c, i, r).start()
-
-    def project(c, k):
-        hidden = gated(slice(k * x_rows, (k + 1) * x_rows), c)
+            for r in range(1, quads):
+                far_copy(c, i, r).start()
+
+    def pass_near(c, i):
+        pass_on(c, i, False)
+
+    def pass_far(c, i):
+        pass_on(c, i, True)
+
+    def project(unit):
+        c, k = unit // LANES, LANES - 1 - unit % LANES
+
+        @pl.when(unit == 0)
+        def _():
+            there = toks.at[pl.ds(x_rows, x_rows), :]
+            pltpu.make_async_copy(there, there, pair_recv.at[0]).wait()
+            pltpu.make_async_copy(there, there, diag_recv.at[0]).wait()
+
+        @pl.when(k == LANES - 1)
+        def _():
+            for _ in range(1, quads):
+                arrived = weights.at[c, pl.ds(0, LANES * height), :]
+                pltpu.make_async_copy(arrived, arrived, far_recv.at[c]).wait()
+
+        h_x[c, k] = gated(pl.ds(pl.multiple_of(k * x_rows, x_rows), x_rows), c)
         slot = lane * chunks + c
-        if k == 0:
-            hid_out[slot, 0:x_rows, :] = hidden
-        else:
-            h_x[c, k - 1] = hidden
-            remote(h_x.at[c, k - 1], hid_out.at[slot, pl.ds(0, x_rows), :], h_send.at[0], h_recv.at[0], fsdp=at_x(k)).start()
+
+        @pl.when(k == 0)
+        def _():
+            hid_out[slot, 0:x_rows, :] = h_x[c, 0]
+
+        @pl.when(k > 0)
+        def _():
+            owner = shard((x_bit + k // 2) % 2, (core + k % 2) % 2)
+            remote(h_x.at[c, k], hid_out.at[slot, pl.ds(0, x_rows), :], h_send.at[0], h_recv.at[0], fsdp=owner).start()
 
     def project_z(c):
         hidden = gated(slice(z_base, z_base + LANES * z_rows), c)
@@ -321,60 +351,65 @@
             remote(h_z.at[c, pl.ds((k - 1) * z_rows, z_rows), :], hid_out.at[slot, pl.ds(x_rows, z_rows), :],
                    h_send.at[1], h_recv.at[1], **z_device(k)).start()
 
-    tail_z = -(-chunks // DOT_LAG)
-
-    @pl.loop(0, chunks + DOT_LAG)
+    tail = -(-DOT_LAG // LANES)
+    tail_z = -(-chunks // (tail - 1))
+    dot_at = jnp.where(at_end, DOT_AT[0], DOT_AT[1])
+
+    def dots_done(n):
+        paced = jnp.maximum(n + 1 - dot_at, 0) * 4 // 3
+        return jnp.clip(jnp.minimum(paced, n + 1 - DOT_LAG), 0, pieces)
+
+    stages = (
+        (gather_in, 0, jnp.logical_not(at_end)), (join, SUM_LAG, at_middle), (update, STEP_LAG, None),
+        (pass_near, NEAR_LAG, None), (pass_far, FAR_LAG, None))
+
+    @pl.loop(0, chunks + tail)
     def _(t):
         for i in range(LANES):
-            @pl.when((t < chunks) & jnp.logical_not(at_end))
-            def _(i=i):
-                gather_in(t, i)
-
-            for stepper, lag, when in ((join, SUM_LAG, at_middle), (update, STEP_LAG, None), (pass_on, PASS_LAG, None)):
+            for stepper, lag, when in stages:
                 c, at = shifted(t, i, lag)
 
                 @pl.when(live(c) if when is None else live(c) & when)
                 def _(stepper=stepper, c=c, at=at):
                     stepper(c, at)
 
-            if LATE_AT % LANES == i:
-                @pl.when(t == LATE_AT // LANES)
+            for role, here in enumerate((at_end, jnp.logical_not(at_end))):
+                for j in range(PARTS):
+                    if SEND_AT[role][j] is not None and SEND_AT[role][j] % LANES == i:
+                        @pl.when((t == SEND_AT[role][j] // LANES) & here)
+                        def _(j=j):
+                            token_x(j).start()
+
+                    if PASS_AT[role][j] % LANES == i:
+                        @pl.when((t == PASS_AT[role][j] // LANES) & here)
+                        def _(j=j):
+                            token_x(j).wait_recv()
+                            token_pass(j).start()
+
+            n = t * LANES + i
+
+            @pl.loop(dots_done(n - 1), dots_done(n))
+            def _(unit):
+                project(unit)
+
+            if i == (SUM_LAG + 1) % LANES:
+                @pl.when((t == chunks + (SUM_LAG + 1) // LANES) & jnp.logical_not(at_end))
                 def _():
-                    for j in range(EARLY, PARTS):
-                        token_x(j).start()
-
-            for j in range(PARTS):
-                if PASS_AT[j] % LANES == i:
-                    @pl.when(t == PASS_AT[j] // LANES)
-                    def _(j=j):
-                        token_x(j).wait_recv()
-                        token_pass(j).start()
-
-            @pl.when(live(t - DOT_LAG))
-            def _(i=i):
-                c = t - DOT_LAG
-                if i == 0:
-                    @pl.when(c == 0)
-                    def _():
-                        there = toks.at[pl.ds(x_rows, x_rows), :]
-                        pltpu.make_async_copy(there, there, pair_recv.at[0]).wait()
-                        pltpu.make_async_copy(there, there, diag_recv.at[0]).wait()
-
-                    for _ in range(1, quads):
-                        arrived = weights.at[c, pl.ds(0, LANES * height), :]
-                        pltpu.make_async_copy(arrived, arrived, far_recv.at[c]).wait()
-                project(c, LANES - 1 - i)
+                    token_z(1).start()
 
         @pl.when(t == chunks)
         def _():
-            token_z().wait_recv()
+            pltpu.make_async_copy(z_part(2), z_part(2), tz_recv).wait()
             token_z_pass().start()
+
+        @pl.when(t == chunks + 1)
+        def _():
             pltpu.make_async_copy(z_part(1), z_part(1), pair_recv.at[1]).wait()
             pltpu.make_async_copy(z_part(3), z_part(3), diag_recv.at[1]).wait()
 
-        @pl.when(t >= chunks)
-        def _():
-            first = (t - chunks) * tail_z
+        @pl.when(t > chunks)
+        def _():
+            first = (t - chunks - 1) * tail_z
 
             @pl.loop(first, jnp.minimum(first + tail_z, chunks))
             def _(c):
@@ -384,7 +419,8 @@
     pltpu.make_async_copy(got, got, h_recv.at[0]).wait()
     got = hid_out.at[pl.ds(0, (LANES - 1) * chunks), pl.ds(x_rows, z_rows), :]
     pltpu.make_async_copy(got, got, h_recv.at[1]).wait()
-    pltpu.make_async_copy(h_x, h_x, h_send.at[0]).wait()
+    sent = h_x.at[:, pl.ds(1, LANES - 1)]
+    pltpu.make_async_copy(sent, sent, h_send.at[0]).wait()
     pltpu.make_async_copy(h_z, h_z, h_send.at[1]).wait()
     pltpu.make_async_copy(own, own, part_send).wait()
 
@@ -446,9 +482,9 @@
                 pltpu.VMEM((chunks, model, 2 * width), bf16),
                 pltpu.VMEM((pieces, height, 2 * width), bf16),
                 strip, strip, strip,
-                pltpu.VMEM((chunks, LANES - 1, x_rows, width), bf16),
+                pltpu.VMEM((chunks, LANES, x_rows, width), bf16),
                 pltpu.VMEM((chunks, (LANES - 1) * z_rows, width), bf16),
-                dma((pieces,)), dma((2,)), dma, dma,
+                dma((pieces,)), dma((PARTS + 1,)), dma, dma,
                 dma((pieces,)), dma((pieces,)), dma((pieces,)), dma, dma,
                 dma((PARTS,)), dma, dma, dma, dma((2,)), dma((2,)), dma,
                 dma((chunks, LANES)), dma, dma((chunks,)), dma, dma((2,)), dma((2,)),

time: 151 us -> 140 us (0.927)
  Pallas kernels: 150 us -> 139 us
    pallas_call x1, Pallas kernels: 143 us -> 131 us  [body(): pl.pallas_call(functools.partial(kernel, groups, shards, z_rows), out_sha...]
where the time goes in v2:
time: 140 us; the launch traced here: 139 us
  Pallas kernels  139 us (99%)
    pallas_call x1, Pallas kernels, body(): pl.pallas_call(functools.partial(kernel, groups, shards, z_rows), out_sha...  131 us
    pallas_call x1, Pallas kernels, body(): pl.pallas_call(store, out_shape=(jax.ShapeDtypeStruct(outer_params.shape,...  7.31 us

profile of v2, /device:TPU:0, one launch (start us, length us, event | category | flops | bytes accessed | tf_op | source)
XLA Modules:
  0.0 139.4 jit_solution(4879234718946564169)
XLA Ops:
  0.6 131.5 %round.1 = (f32[2,256,4096]{2,1,0:T(8,128)S(1)}, f32[2,256,4096]{2,1,0:T(8,128)S(1)}, bf16[32,512,128]{2,1,0:T(8,128)(2,1)S(1)}) custom-call(bf16[512,2048]{1,0:T(8,128)(2,1)} %tokens.1, f32[1,2048]{1,0:T(1,128)} %bitcast.1, f32[2,256,4096]{2,1,0:T(8,128)} %params.1, f32[2,256,4096]{2,1,0:T(8,128)} %moment.1, bf16[1,2,256,4096]{3,2,1,0:T(8,128)(2,1)} %deltas.1), custom_call_target="tpu_custom_call" | custom-call | tf_op jit(solution)/shard_map/round/pallas_call | solution.py:471
  132.1 7.3 %store.1 = (f32[2,256,4096]{2,1,0:T(8,128)}, f32[2,256,4096]{2,1,0:T(8,128)}, bf16[512,4096]{1,0:T(8,128)(2,1)}) custom-call(f32[2,256,4096]{2,1,0:T(8,128)S(1)} %get-tuple-element.6.p_in, f32[2,256,4096]{2,1,0:T(8,128)S(1)} %get-tuple-element.7.m_in, bf16[32,512,128]{2,1,0:T(8,128)(2,1)S(1)} %get-tuple-element.8.h_in), custom_call_target="tpu_custom_call" | custom-call | tf_op jit(solution)/shard_map/store/pallas_call | solution.py:496

commit v3 on v2

--- a/solution.py
+++ b/solution.py
@@ -15,14 +15,15 @@
 LANES = 4
 WIDTH = 128
 PARTS = 6
-SEND_AT = ((None, None, None, None, 5, 9), (None, None, 3, 7, 11, 15))
-PASS_AT = ((2, 4, 6, 8, 10, 13), (2, 4, 8, 12, 15, 19))
-DOT_AT = (14, 20)
+SEND_AT = ((None, None, None, None, 4, 8), (None, None, 2, 6, 10, 14))
+PASS_AT = ((2, 4, 6, 8, 10, 14), (2, 4, 8, 12, 16, 19))
+DOT_AT = (15, 20)
+Z_PARTS = 4
+Z_EARLY = 2
 SUM_LAG = 1
-STEP_LAG = 2
-NEAR_LAG = 4
+NEAR_LAG = 3
 FAR_LAG = 5
-DOT_LAG = 12
+DOT_LAG = (10, 12)
 
 
 def advance(params, moment, summed, groups):
@@ -126,10 +127,10 @@
     def x_part(k, j):
         return toks.at[pl.ds(k * x_rows + j * part_rows, part_rows), :]
 
-    def z_part(k, half=None):
-        if half is None:
+    def z_part(k, j=None):
+        if j is None:
             return toks.at[pl.ds(z_base + k * z_rows, z_rows), :]
-        return toks.at[pl.ds(z_base + k * z_rows + half * (z_rows // 2), z_rows // 2), :]
+        return toks.at[pl.ds(z_base + k * z_rows + j * (z_rows // Z_PARTS), z_rows // Z_PARTS), :]
 
     def token_x(j):
         return remote(x_part(0, j), x_part(2, j), tx_send, tx_recv.at[j], fsdp=at_x(2))
@@ -137,8 +138,8 @@
     def token_pass(j):
         return remote(x_part(2, j), x_part(3, j), pair_send, diag_recv.at[0], fsdp=at_x(1))
 
-    def token_z(half):
-        return remote(z_part(0, half), z_part(2, half), tz_send, tz_recv, rep=z_pair)
+    def token_z(j):
+        return remote(z_part(0, j), z_part(2, j), tz_send, tz_recv, rep=z_pair)
 
     def token_z_pass():
         return remote(z_part(2), z_part(3), pair_send, diag_recv.at[1], fsdp=at_x(1))
@@ -219,11 +220,13 @@
 
     token_copies[PARTS].wait()
     normalize(z_base, z_rows)
-    token_z(0).start()
+    for j in range(Z_EARLY):
+        token_z(j).start()
 
     @pl.when(at_end)
     def _():
-        token_z(1).start()
+        for j in range(Z_EARLY, Z_PARTS):
+            token_z(j).start()
 
     remote(toks.at[pl.ds(0, x_rows), :], toks.at[pl.ds(x_rows, x_rows), :], pair_send, pair_recv.at[0], fsdp=at_x(1)).start()
     remote(z_part(0), z_part(1), pair_send, pair_recv.at[1], fsdp=at_x(1)).start()
@@ -323,6 +326,7 @@
             there = toks.at[pl.ds(x_rows, x_rows), :]
             pltpu.make_async_copy(there, there, pair_recv.at[0]).wait()
             pltpu.make_async_copy(there, there, diag_recv.at[0]).wait()
+            pltpu.make_async_copy(z_part(1), z_part(1), pair_recv.at[1]).wait()
 
         @pl.when(k == LANES - 1)
         def _():
@@ -336,84 +340,99 @@
         @pl.when(k == 0)
         def _():
             hid_out[slot, 0:x_rows, :] = h_x[c, 0]
+            project_z_near(c)
 
         @pl.when(k > 0)
         def _():
             owner = shard((x_bit + k // 2) % 2, (core + k % 2) % 2)
             remote(h_x.at[c, k], hid_out.at[slot, pl.ds(0, x_rows), :], h_send.at[0], h_recv.at[0], fsdp=owner).start()
 
-    def project_z(c):
-        hidden = gated(slice(z_base, z_base + LANES * z_rows), c)
+    def send_z(c, k, slot):
+        remote(h_z.at[c, k - 1], hid_out.at[slot, pl.ds(x_rows, z_rows), :], h_send.at[1], h_recv.at[1], **z_device(k)).start()
+
+    def project_z_near(c):
+        hidden = gated(slice(z_base, z_base + 2 * z_rows), c)
         slot = lane * chunks + c
+        h_z[c, 0] = hidden[z_rows:]
+        send_z(c, 1, slot)
         hid_out[slot, x_rows:rows, :] = hidden[0:z_rows]
-        h_z[c] = hidden[z_rows:]
-        for k in (3, 2, 1):
-            remote(h_z.at[c, pl.ds((k - 1) * z_rows, z_rows), :], hid_out.at[slot, pl.ds(x_rows, z_rows), :],
-                   h_send.at[1], h_recv.at[1], **z_device(k)).start()
-
-    tail = -(-DOT_LAG // LANES)
-    tail_z = -(-chunks // (tail - 1))
+
+    def project_z_far(c):
+        hidden = gated(slice(z_base + 2 * z_rows, z_base + 4 * z_rows), c)
+        slot = lane * chunks + c
+        h_z[c, 1] = hidden[0:z_rows]
+        h_z[c, 2] = hidden[z_rows:]
+        send_z(c, 3, slot)
+        send_z(c, 2, slot)
+
+    tail = -(-max(DOT_LAG) // LANES)
     dot_at = jnp.where(at_end, DOT_AT[0], DOT_AT[1])
+    dot_lag = jnp.where(at_end, DOT_LAG[0], DOT_LAG[1])
 
     def dots_done(n):
         paced = jnp.maximum(n + 1 - dot_at, 0) * 4 // 3
-        return jnp.clip(jnp.minimum(paced, n + 1 - DOT_LAG), 0, pieces)
-
-    stages = (
-        (gather_in, 0, jnp.logical_not(at_end)), (join, SUM_LAG, at_middle), (update, STEP_LAG, None),
-        (pass_near, NEAR_LAG, None), (pass_far, FAR_LAG, None))
+        return jnp.clip(jnp.minimum(paced, n + 1 - dot_lag), 0, pieces)
+
+    def on_pieces(t, i, *stages):
+        for stepper, lag, when in stages:
+            c, at = shifted(t, i, lag)
+
+            @pl.when(live(c) if when is None else live(c) & when)
+            def _(stepper=stepper, c=c, at=at):
+                stepper(c, at)
+
+    def on_tokens(t, i, table, act):
+        for here, steps in zip((at_end, jnp.logical_not(at_end)), table):
+            for j, step in enumerate(steps):
+                if step is not None and step % LANES == i:
+                    @pl.when((t == step // LANES) & here)
+                    def _(j=j):
+                        act(j)
+
+    def pass_token(j):
+        token_x(j).wait_recv()
+        token_pass(j).start()
+
+    def send_token(j):
+        token_x(j).start()
 
     @pl.loop(0, chunks + tail)
     def _(t):
         for i in range(LANES):
-            for stepper, lag, when in stages:
-                c, at = shifted(t, i, lag)
-
-                @pl.when(live(c) if when is None else live(c) & when)
-                def _(stepper=stepper, c=c, at=at):
-                    stepper(c, at)
-
-            for role, here in enumerate((at_end, jnp.logical_not(at_end))):
-                for j in range(PARTS):
-                    if SEND_AT[role][j] is not None and SEND_AT[role][j] % LANES == i:
-                        @pl.when((t == SEND_AT[role][j] // LANES) & here)
-                        def _(j=j):
-                            token_x(j).start()
-
-                    if PASS_AT[role][j] % LANES == i:
-                        @pl.when((t == PASS_AT[role][j] // LANES) & here)
-                        def _(j=j):
-                            token_x(j).wait_recv()
-                            token_pass(j).start()
-
             n = t * LANES + i
+            on_pieces(t, i, (gather_in, 0, jnp.logical_not(at_end)), (pass_near, NEAR_LAG, None), (pass_far, FAR_LAG, None))
+            on_tokens(t, i, PASS_AT, pass_token)
 
             @pl.loop(dots_done(n - 1), dots_done(n))
             def _(unit):
                 project(unit)
 
-            if i == (SUM_LAG + 1) % LANES:
-                @pl.when((t == chunks + (SUM_LAG + 1) // LANES) & jnp.logical_not(at_end))
+            on_pieces(t, i, (join, SUM_LAG, at_middle), (update, SUM_LAG, None))
+            on_tokens(t, i, SEND_AT, send_token)
+
+            if i == LANES - 2:
+                @pl.when(t == chunks)
                 def _():
-                    token_z(1).start()
-
-        @pl.when(t == chunks)
-        def _():
-            pltpu.make_async_copy(z_part(2), z_part(2), tz_recv).wait()
-            token_z_pass().start()
-
-        @pl.when(t == chunks + 1)
-        def _():
-            pltpu.make_async_copy(z_part(1), z_part(1), pair_recv.at[1]).wait()
+                    pltpu.make_async_copy(z_part(2), z_part(2), tz_recv).wait()
+                    token_z_pass().start()
+
+            if i == SUM_LAG:
+                @pl.when((t == chunks) & jnp.logical_not(at_end))
+                def _():
+                    for j in range(Z_EARLY, Z_PARTS):
+                        token_z(j).start()
+
+        bulk = jnp.where(at_end, chunks, chunks + 1)
+
+        @pl.when(t == bulk)
+        def _():
             pltpu.make_async_copy(z_part(3), z_part(3), diag_recv.at[1]).wait()
 
-        @pl.when(t > chunks)
-        def _():
-            first = (t - chunks - 1) * tail_z
-
-            @pl.loop(first, jnp.minimum(first + tail_z, chunks))
-            def _(c):
-                project_z(c)
+        final = chunks + tail - 1
+
+        @pl.loop(jnp.where(t == final, chunks - 1, 0), jnp.where(t == bulk, chunks - 1, jnp.where(t == final, chunks, 0)))
+        def _(c):
+            project_z_far(c)
 
     got = hid_out.at[pl.ds(0, (LANES - 1) * chunks), pl.ds(0, x_rows), :]
     pltpu.make_async_copy(got, got, h_recv.at[0]).wait()
@@ -483,7 +502,7 @@
                 pltpu.VMEM((pieces, height, 2 * width), bf16),
                 strip, strip, strip,
                 pltpu.VMEM((chunks, LANES, x_rows, width), bf16),
-                pltpu.VMEM((chunks, (LANES - 1) * z_rows, width), bf16),
+                pltpu.VMEM((chunks, LANES - 1, z_rows, width), bf16),
                 dma((pieces,)), dma((PARTS + 1,)), dma, dma,
                 dma((pieces,)), dma((pieces,)), dma((pieces,)), dma, dma,
                 dma((PARTS,)), dma, dma, dma, dma((2,)), dma((2,)), dma,

time: 140 us -> 137 us (0.979)
  Pallas kernels: 139 us -> 136 us
    pallas_call x1, Pallas kernels: 131 us -> 129 us  [body(): pl.pallas_call(functools.partial(kernel, groups, shards, z_rows), out_sha...]
where the time goes in v3:
time: 137 us
  Pallas kernels  136 us (99%)
    pallas_call x1, Pallas kernels, body(): pl.pallas_call(functools.partial(kernel, groups, shards, z_rows), out_sha...  129 us
    pallas_call x1, Pallas kernels, body(): pl.pallas_call(store, out_shape=(jax.ShapeDtypeStruct(outer_params.shape,...  7.31 us

profile of v3, /device:TPU:0, one launch (start us, length us, event | category | flops | bytes accessed | tf_op | source)
XLA Modules:
  0.0 136.8 jit_solution(5469554213658215479)
XLA Ops:
  0.6 128.8 %round.1 = (f32[2,256,4096]{2,1,0:T(8,128)S(1)}, f32[2,256,4096]{2,1,0:T(8,128)S(1)}, bf16[32,512,128]{2,1,0:T(8,128)(2,1)S(1)}) custom-call(bf16[512,2048]{1,0:T(8,128)(2,1)} %tokens.1, f32[1,2048]{1,0:T(1,128)} %bitcast.1, f32[2,256,4096]{2,1,0:T(8,128)} %params.1, f32[2,256,4096]{2,1,0:T(8,128)} %moment.1, bf16[1,2,256,4096]{3,2,1,0:T(8,128)(2,1)} %deltas.1), custom_call_target="tpu_custom_call" | custom-call | tf_op jit(solution)/shard_map/round/pallas_call | solution.py:490
  129.5 7.3 %store.1 = (f32[2,256,4096]{2,1,0:T(8,128)}, f32[2,256,4096]{2,1,0:T(8,128)}, bf16[512,4096]{1,0:T(8,128)(2,1)}) custom-call(f32[2,256,4096]{2,1,0:T(8,128)S(1)} %get-tuple-element.6.p_in, f32[2,256,4096]{2,1,0:T(8,128)S(1)} %get-tuple-element.7.m_in, bf16[32,512,128]{2,1,0:T(8,128)(2,1)S(1)} %get-tuple-element.8.h_in), custom_call_target="tpu_custom_call" | custom-call | tf_op jit(solution)/shard_map/store/pallas_call | solution.py:515

commit v4 on v3

--- a/solution.py
+++ b/solution.py
@@ -22,7 +22,7 @@
 Z_EARLY = 2
 SUM_LAG = 1
 NEAR_LAG = 3
-FAR_LAG = 5
+FAR_LAG = (5, 6)
 DOT_LAG = (10, 12)
 
 
@@ -127,10 +127,15 @@
     def x_part(k, j):
         return toks.at[pl.ds(k * x_rows + j * part_rows, part_rows), :]
 
-    def z_part(k, j=None):
-        if j is None:
-            return toks.at[pl.ds(z_base + k * z_rows, z_rows), :]
-        return toks.at[pl.ds(z_base + k * z_rows + j * (z_rows // Z_PARTS), z_rows // Z_PARTS), :]
+    z_half = z_rows // 2
+    z_quarter = z_rows // Z_PARTS
+    far_base = z_base + 2 * z_rows
+
+    def z_part(k):
+        return toks.at[pl.ds(z_base + k * z_rows, z_rows), :]
+
+    def z_far(k, h):
+        return toks.at[pl.ds(far_base + h * z_rows + (k - 2) * z_half, z_half), :]
 
     def token_x(j):
         return remote(x_part(0, j), x_part(2, j), tx_send, tx_recv.at[j], fsdp=at_x(2))
@@ -139,10 +144,31 @@
         return remote(x_part(2, j), x_part(3, j), pair_send, diag_recv.at[0], fsdp=at_x(1))
 
     def token_z(j):
-        return remote(z_part(0, j), z_part(2, j), tz_send, tz_recv, rep=z_pair)
-
-    def token_z_pass():
-        return remote(z_part(2), z_part(3), pair_send, diag_recv.at[1], fsdp=at_x(1))
+        h, within = j // (Z_PARTS // 2), j % (Z_PARTS // 2)
+        src = toks.at[pl.ds(z_base + j * z_quarter, z_quarter), :]
+        dst = toks.at[pl.ds(far_base + h * z_rows + within * z_quarter, z_quarter), :]
+        return remote(src, dst, tz_send, tz_recv.at[h], rep=z_pair)
+
+    def pass_z(h):
+        pltpu.make_async_copy(z_far(2, h), z_far(2, h), tz_recv.at[h]).wait()
+        remote(z_far(2, h), z_far(3, h), pair_send, diag_recv.at[1 + h], fsdp=at_x(1)).start()
+
+    def passed_z(h):
+        pltpu.make_async_copy(z_far(3, h), z_far(3, h), diag_recv.at[1 + h]).wait()
+
+    barrier = pltpu.get_barrier_semaphore()
+    for k in (1, 2, 3):
+        pl.semaphore_signal(barrier, inc=1, device_id={"fsdp": at_x(k)}, device_id_type=pl.DeviceIdType.MESH)
+    for r in range(1, quads):
+        pl.semaphore_signal(
+            barrier, inc=1, device_id={"fsdp": shard(x_bit, core, (quad + r) % quads)}, device_id_type=pl.DeviceIdType.MESH)
+    pl.semaphore_signal(barrier, inc=1, device_id=z_device(3), device_id_type=pl.DeviceIdType.MESH)
+    pl.semaphore_signal(barrier, inc=1, device_id={"rep": inward}, device_id_type=pl.DeviceIdType.MESH)
+    greeted = LANES - 1 + quads - 1 + 2
+
+    @pl.when(jnp.logical_not(at_end))
+    def _():
+        pl.semaphore_signal(barrier, inc=1, device_id={"rep": outward}, device_id_type=pl.DeviceIdType.MESH)
 
     @pl.loop(0, chunks)
     def _(c):
@@ -162,21 +188,6 @@
     p_load.start()
     m_load.start()
 
-    barrier = pltpu.get_barrier_semaphore()
-    greeted = 0
-    for k in (1, 2, 3):
-        pl.semaphore_signal(barrier, inc=1, device_id={"fsdp": at_x(k)}, device_id_type=pl.DeviceIdType.MESH)
-    for r in range(1, quads):
-        pl.semaphore_signal(
-            barrier, inc=1, device_id={"fsdp": shard(x_bit, core, (quad + r) % quads)}, device_id_type=pl.DeviceIdType.MESH)
-    pl.semaphore_signal(barrier, inc=1, device_id=z_device(3), device_id_type=pl.DeviceIdType.MESH)
-    pl.semaphore_signal(barrier, inc=1, device_id={"rep": inward}, device_id_type=pl.DeviceIdType.MESH)
-    greeted = LANES - 1 + quads - 1 + 2
-
-    @pl.when(jnp.logical_not(at_end))
-    def _():
-        pl.semaphore_signal(barrier, inc=1, device_id={"rep": outward}, device_id_type=pl.DeviceIdType.MESH)
-
     @pl.when(jnp.logical_not(at_end))
     def _():
         pl.semaphore_wait(barrier, greeted + 1)
@@ -328,6 +339,10 @@
             pltpu.make_async_copy(there, there, diag_recv.at[0]).wait()
             pltpu.make_async_copy(z_part(1), z_part(1), pair_recv.at[1]).wait()
 
+            @pl.when(at_end)
+            def _():
+                passed_z(0)
+
         @pl.when(k == LANES - 1)
         def _():
             for _ in range(1, quads):
@@ -342,28 +357,44 @@
             hid_out[slot, 0:x_rows, :] = h_x[c, 0]
             project_z_near(c)
 
+            @pl.when(at_end)
+            def _():
+                project_z_far(c, 0)
+
         @pl.when(k > 0)
         def _():
             owner = shard((x_bit + k // 2) % 2, (core + k % 2) % 2)
             remote(h_x.at[c, k], hid_out.at[slot, pl.ds(0, x_rows), :], h_send.at[0], h_recv.at[0], fsdp=owner).start()
 
-    def send_z(c, k, slot):
-        remote(h_z.at[c, k - 1], hid_out.at[slot, pl.ds(x_rows, z_rows), :], h_send.at[1], h_recv.at[1], **z_device(k)).start()
+        @pl.when((c == chunks - 1) & (k == 2))
+        def _():
+            project_z_rest(c)
+
+    def send_z(c, k, first, count):
+        slot = lane * chunks + c
+        remote(h_z.at[c, k - 1, pl.ds(first, count), :], hid_out.at[slot, pl.ds(x_rows + first, count), :],
+               h_send.at[1], h_recv.at[1], **z_device(k)).start()
 
     def project_z_near(c):
-        hidden = gated(slice(z_base, z_base + 2 * z_rows), c)
-        slot = lane * chunks + c
+        hidden = gated(slice(z_base, far_base), c)
         h_z[c, 0] = hidden[z_rows:]
-        send_z(c, 1, slot)
-        hid_out[slot, x_rows:rows, :] = hidden[0:z_rows]
-
-    def project_z_far(c):
-        hidden = gated(slice(z_base + 2 * z_rows, z_base + 4 * z_rows), c)
-        slot = lane * chunks + c
-        h_z[c, 1] = hidden[0:z_rows]
-        h_z[c, 2] = hidden[z_rows:]
-        send_z(c, 3, slot)
-        send_z(c, 2, slot)
+        send_z(c, 1, 0, z_rows)
+        hid_out[lane * chunks + c, x_rows:rows, :] = hidden[0:z_rows]
+
+    def project_z_far(c, h):
+        hidden = gated(slice(far_base + h * z_rows, far_base + (h + 1) * z_rows), c)
+        at = slice(h * z_half, (h + 1) * z_half)
+        h_z[c, 1, at, :] = hidden[0:z_half]
+        h_z[c, 2, at, :] = hidden[z_half:]
+        for k in (3, 2):
+            send_z(c, k, h * z_half, z_half)
+
+    def project_z_rest(c):
+        @pl.when(jnp.logical_not(at_end))
+        def _():
+            project_z_far(c, 0)
+
+        project_z_far(c, 1)
 
     tail = -(-max(DOT_LAG) // LANES)
     dot_at = jnp.where(at_end, DOT_AT[0], DOT_AT[1])
@@ -400,7 +431,7 @@
     def _(t):
         for i in range(LANES):
             n = t * LANES + i
-            on_pieces(t, i, (gather_in, 0, jnp.logical_not(at_end)), (pass_near, NEAR_LAG, None), (pass_far, FAR_LAG, None))
+            on_pieces(t, i, (gather_in, 0, jnp.logical_not(at_end)), (pass_near, NEAR_LAG, None), (pass_far, FAR_LAG[0], at_end), (pass_far, FAR_LAG[1], jnp.logical_not(at_end)))
             on_tokens(t, i, PASS_AT, pass_token)
 
             @pl.loop(dots_done(n - 1), dots_done(n))
@@ -410,11 +441,14 @@
             on_pieces(t, i, (join, SUM_LAG, at_middle), (update, SUM_LAG, None))
             on_tokens(t, i, SEND_AT, send_token)
 
-            if i == LANES - 2:
+            if i == LANES - 1:
+                @pl.when(t == jnp.where(at_end, 1, chunks))
+                def _():
+                    pass_z(0)
+
                 @pl.when(t == chunks)
                 def _():
-                    pltpu.make_async_copy(z_part(2), z_part(2), tz_recv).wait()
-                    token_z_pass().start()
+                    pass_z(1)
 
             if i == SUM_LAG:
                 @pl.when((t == chunks) & jnp.logical_not(at_end))
@@ -422,17 +456,17 @@
                     for j in range(Z_EARLY, Z_PARTS):
                         token_z(j).start()
 
-        bulk = jnp.where(at_end, chunks, chunks + 1)
-
-        @pl.when(t == bulk)
-        def _():
-            pltpu.make_async_copy(z_part(3), z_part(3), diag_recv.at[1]).wait()
-
-        final = chunks + tail - 1
-
-        @pl.loop(jnp.where(t == final, chunks - 1, 0), jnp.where(t == bulk, chunks - 1, jnp.where(t == final, chunks, 0)))
-        def _(c):
-            project_z_far(c)
+        @pl.when(t == jnp.where(at_end, chunks, chunks + 1))
+        def _():
+            @pl.when(jnp.logical_not(at_end))
+            def _():
+                passed_z(0)
+
+            passed_z(1)
+
+            @pl.loop(0, chunks - 1)
+            def _(c):
+                project_z_rest(c)
 
     got = hid_out.at[pl.ds(0, (LANES - 1) * chunks), pl.ds(0, x_rows), :]
     pltpu.make_async_copy(got, got, h_recv.at[0]).wait()
@@ -464,8 +498,12 @@
     m_copy = pltpu.make_async_copy(m_in, m_out, m_sem)
     for j in range(blocks):
         pltpu.make_async_copy(h_in.at[j], hidden.at[:, pl.ds(j * width, width)], h_sem).start()
-    p_copy.start()
-    m_copy.start()
+    for src, dst, sem in ((p_in, p_out, p_sem), (m_in, m_out, m_sem)):
+        which, height, _ = src.shape
+        for w in range(which):
+            for r in range(4):
+                at = pl.ds(r * (height // 4), height // 4)
+                pltpu.make_async_copy(src.at[w, at], dst.at[w, at], sem).start()
     pltpu.make_async_copy(h_in, h_in, h_sem).wait()
     p_copy.wait()
     m_copy.wait()
@@ -505,7 +543,7 @@
                 pltpu.VMEM((chunks, LANES - 1, z_rows, width), bf16),
                 dma((pieces,)), dma((PARTS + 1,)), dma, dma,
                 dma((pieces,)), dma((pieces,)), dma((pieces,)), dma, dma,
-                dma((PARTS,)), dma, dma, dma, dma((2,)), dma((2,)), dma,
+                dma((PARTS,)), dma, dma((2,)), dma, dma((2,)), dma((3,)), dma,
                 dma((chunks, LANES)), dma, dma((chunks,)), dma, dma((2,)), dma((2,)),
             ],
             compiler_params=pltpu.CompilerParams(

time: 137 us -> 136 us (level)
  no operation moved by 1% of the time
where the time goes in v4:
time: 136 us
  Pallas kernels  135 us (99%)
    pallas_call x1, Pallas kernels, body(): pl.pallas_call(functools.partial(kernel, groups, shards, z_rows), out_sha...  128 us
    pallas_call x1, Pallas kernels, body(): pl.pallas_call(store, out_shape=(jax.ShapeDtypeStruct(outer_params.shape,...  7.1 us

profile of v4, /device:TPU:0, one launch (start us, length us, event | category | flops | bytes accessed | tf_op | source)
XLA Modules:
  0.0 135.9 jit_solution(14329954589150800524)
XLA Ops:
  0.6 128.2 %round.1 = (f32[2,256,4096]{2,1,0:T(8,128)S(1)}, f32[2,256,4096]{2,1,0:T(8,128)S(1)}, bf16[32,512,128]{2,1,0:T(8,128)(2,1)S(1)}) custom-call(bf16[512,2048]{1,0:T(8,128)(2,1)} %tokens.1, f32[1,2048]{1,0:T(1,128)} %bitcast.1, f32[2,256,4096]{2,1,0:T(8,128)} %params.1, f32[2,256,4096]{2,1,0:T(8,128)} %moment.1, bf16[1,2,256,4096]{3,2,1,0:T(8,128)(2,1)} %deltas.1), custom_call_target="tpu_custom_call" | custom-call | tf_op jit(solution)/shard_map/round/pallas_call | solution.py:528
  128.8 7.1 %store.1 = (f32[2,256,4096]{2,1,0:T(8,128)}, f32[2,256,4096]{2,1,0:T(8,128)}, bf16[512,4096]{1,0:T(8,128)(2,1)}) custom-call(f32[2,256,4096]{2,1,0:T(8,128)S(1)} %get-tuple-element.6.p_in, f32[2,256,4096]{2,1,0:T(8,128)S(1)} %get-tuple-element.7.m_in, bf16[32,512,128]{2,1,0:T(8,128)(2,1)S(1)} %get-tuple-element.8.h_in), custom_call_target="tpu_custom_call" | custom-call | tf_op jit(solution)/shard_map/store/pallas_call | solution.py:553
